TPU v7x, 32 devices: a whole 2x2x4 slice. The times are simulated.
32 devices in a mesh: outer: 4 (over y, core), inner: 8 (over z, x).
Axes of the slice: x: 2, y: 2, z: 4, core: 2. Of those that a mesh axis runs over, the one named last changes fastest.
Arguments:
- tokens: bfloat16 [12288, 4096], P(('outer', 'inner')), may hold values from -6 to 6
- out_grad: bfloat16 [12288, 1024], P(('outer', 'inner')), may hold values from -0.3125 to 0.3125
- master_weights: float32 [1024, 4096], P(('outer', 'inner')), may hold values from -0.0421 to 0.0421
- base_weights: bfloat16 [1024, 4096], replicated, may hold values from -0.030029297 to 0.030029297
- adam_m: float32 [1024, 4096], P(('outer', 'inner')), may hold values from -8 to 8
- adam_v: float32 [1024, 4096], P(('outer', 'inner')), may hold values from 0.1 to 10
- grad_exps: int32 [32, 8, 32], P(('outer', 'inner')), may hold values from -13 to -8
- diff_exps: int32 [1024, 32], P(('outer', 'inner')), may hold values from -20 to -15
- hadamard_signs: int32 [32, 128], replicated, may hold values 0 or 1
Outputs:
- projected: bfloat16 [12288, 1024], P(('outer', 'inner'))
- new_master: float32 [1024, 4096], P(('outer', 'inner'))
- new_first: float32 [1024, 4096], P(('outer', 'inner'))
- new_second: float32 [1024, 4096], P(('outer', 'inner'))
All inputs are finite; a program needn't handle non-finite values.
Results may differ from a plain program's by a relative error of at most 0.005.
Values may be sent and summed in bfloat16 or wider, within the bound.
A program may use at most 128 MiB of HBM per device.

v0:
```python
import functools
import math

import jax
import jax.numpy as jnp
import numpy as np
from jax import lax
from jax.experimental import pallas as pl
from jax.experimental.pallas import tpu as pltpu
from jax.sharding import PartitionSpec as P

ADAM_STEP = 10


clip_level = 448.0
beta_one = 0.9
beta_two = 0.95
learn_rate = 0.002
decay_rate = 0.1
adam_eps = 1e-08
highest = lax.Precision.HIGHEST


def hadamard(matrix_size):
    positions = jnp.arange(matrix_size, dtype=jnp.int32)
    common = positions[:, None] & positions[None, :]
    parity = jnp.zeros((matrix_size, matrix_size), jnp.int32)
    for bit_level in range(matrix_size.bit_length() - 1):
        parity = parity + (common >> bit_level & 1)
    return (1 - 2 * (parity % 2)).astype(jnp.float32)


def rotate_rows(row_block, sign_rows, matrix):
    row_count = row_block.shape[0]
    blocks = row_block.reshape(row_count, sign_rows.shape[0], sign_rows.shape[1]) * sign_rows
    turned = jnp.dot(blocks.reshape(-1, sign_rows.shape[1]), matrix, precision=highest)
    return turned.reshape(row_block.shape) / math.sqrt(sign_rows.shape[1])


def unrotate_rows(row_block, sign_rows, matrix):
    row_count = row_block.shape[0]
    turned = jnp.dot(
        row_block.reshape(-1, sign_rows.shape[1]), matrix, precision=highest
    ) / math.sqrt(sign_rows.shape[1])
    return (turned.reshape(row_count, sign_rows.shape[0], sign_rows.shape[1]) * sign_rows).reshape(
        row_block.shape
    )


def clip_rows(row_block, bound_rows):
    row_count = row_block.shape[0]
    shaped = row_block.reshape(row_count, bound_rows.shape[1], -1)
    limits = bound_rows[:, :, None]
    return jnp.clip(shaped, -limits, limits).reshape(row_block.shape)


def adam_update(gradient, master, first, second):
    new_first = beta_one * first + (1.0 - beta_one) * gradient
    new_second = beta_two * second + (1.0 - beta_two) * gradient * gradient
    fix_one = 1.0 - beta_one**ADAM_STEP
    fix_two = 1.0 - beta_two**ADAM_STEP
    step_dir = new_first / fix_one / (jnp.sqrt(new_second / fix_two) + adam_eps)
    new_master = master - learn_rate * (step_dir + decay_rate * master)
    return (new_master, new_first, new_second)


CHUNKS = 8
MESH = pl.DeviceIdType.MESH


def step_kernel(
    chunks,
    tokens,
    grad_rows,
    master,
    base_hbm,
    first,
    second,
    bounds,
    diff_bounds,
    signs,
    matrix_half,
    matrix,
    projected,
    out_gradient,
    base,
    grad_t,
    coded,
    rec0,
    sum0,
    rec1,
    sum1,
    rec2,
    sum2,
    rec3,
    gath,
    turned,
    effective,
    total,
    base_sem,
    send_sem,
    recv_sem,
    zsend,
    zrecv,
):
    outer, inner = lax.axis_index("outer"), lax.axis_index("inner")
    inner_count = lax.axis_size("inner")
    xs = 2
    zs = inner_count // xs
    y, c = outer // 2, outer % 2
    z, x = inner // xs, inner % xs
    rows = master.shape[0]
    width = tokens.shape[1] // chunks
    block_len = matrix.shape[0]
    blocks = width // block_len
    row_blocks = grad_t.shape[0] // block_len
    z_step = block_len // (xs * rows)
    scale = 1.0 / math.sqrt(block_len)
    mine1 = x * (1 - c) + y * c
    mine2 = y * (1 - c) + x * c
    core_peer = (y * 2 + 1 - c, inner)
    x_peer = (outer, z * xs + 1 - x)
    y_peer = ((1 - y) * 2 + c, inner)
    peer1 = (x_peer[0] * (1 - c) + y_peer[0] * c, x_peer[1] * (1 - c) + y_peer[1] * c)
    peer2 = (y_peer[0] * (1 - c) + x_peer[0] * c, y_peer[1] * (1 - c) + x_peer[1] * c)
    z_ids = [lax.rem(z + k, zs) for k in range(1, zs)]
    z_peers = [(outer, zz * xs + x) for zz in z_ids]

    load_base = pltpu.make_async_copy(base_hbm, base, base_sem)
    load_base.start()
    barrier = pltpu.get_barrier_semaphore()
    peers = [core_peer, peer1, peer2] + z_peers
    for peer in peers:
        pl.semaphore_signal(barrier, inc=1, device_id=peer, device_id_type=MESH)
    grad_t[...] = grad_rows[...].T
    total[...] = jnp.zeros_like(total)
    pl.semaphore_wait(barrier, len(peers))

    def remote(src, dst, stage, j, peer):
        return pltpu.make_async_remote_copy(
            src_ref=src,
            dst_ref=dst,
            send_sem=send_sem.at[stage, j],
            recv_sem=recv_sem.at[stage, j],
            device_id=peer,
            device_id_type=MESH,
        )

    def remote_z(src, dst, stage, j, k):
        return pltpu.make_async_remote_copy(
            src_ref=src,
            dst_ref=dst,
            send_sem=zsend.at[stage, j, k],
            recv_sem=zrecv.at[stage, j, k],
            device_id=z_peers[k],
            device_id_type=MESH,
        )

    def copy0(j):
        return remote(coded.at[j, 1 - c], rec0.at[j], 0, j, core_peer)

    def copy1(j):
        return remote(sum0.at[j, 1 - mine1], rec1.at[j], 1, j, peer1)

    def copy2(j):
        return remote(sum1.at[j, 1 - mine2], rec2.at[j], 2, j, peer2)

    def copy3(j):
        return [remote_z(sum2.at[j, z_ids[k]], rec3.at[j, k], 0, j, k) for k in range(zs - 1)]

    def gather0(j):
        block = gath.at[j, c, mine1, mine2, z]
        return [remote_z(block, block, 1, j, k) for k in range(zs - 1)]

    def gather1(j):
        block = gath.at[j, c, mine1, mine2]
        return remote(block, block, 3, j, peer2)

    def gather2(j):
        block = gath.at[j, c, mine1]
        return remote(block, block, 4, j, peer1)

    def gather3(j):
        block = gath.at[j, c]
        return remote(block, block, 5, j, core_peer)

    def added(left, right):
        return (left.astype(jnp.float32) + right.astype(jnp.float32)).astype(jnp.bfloat16)

    def columns(j):
        return pl.ds(pl.multiple_of(j * width, width), width)

    def produce(j):
        for b in range(blocks):
            at = pl.ds(pl.multiple_of(j * width + b * block_len, block_len), block_len)
            part = jnp.dot(
                tokens[:, at] * signs[:, at].astype(jnp.bfloat16),
                matrix_half[...],
                preferred_element_type=jnp.float32,
            )
            turned[:, b * block_len : (b + 1) * block_len] = (part * scale).astype(jnp.bfloat16)

        def one(m, carry):
            part = jnp.dot(
                grad_t[pl.ds(pl.multiple_of(m * block_len, block_len), block_len), :],
                turned[...],
                preferred_element_type=jnp.float32,
            )
            limit = bounds[pl.ds(m, 1), columns(j)]
            part = jnp.minimum(jnp.maximum(part, -limit), limit).astype(jnp.bfloat16)
            per = row_blocks // 4
            group = m // per
            z0 = (m - group * per) * z_step
            coded[j, group % 2, group // 2, pl.ds(z0, z_step)] = part.reshape(
                z_step, xs, rows, width
            )
            return carry

        lax.fori_loop(0, row_blocks, one, 0)
        copy0(j).start()

    def reduce0(j):
        copy0(j).wait()
        for yy in range(2):
            for zz in range(zs):
                for xx in range(xs):
                    to1 = xx * (1 - c) + yy * c
                    to2 = yy * (1 - c) + xx * c
                    sum0[j, to1, to2, zz] = added(coded[j, c, yy, zz, xx], rec0[j, yy, zz, xx])
        copy1(j).start()

    def reduce1(j):
        copy1(j).wait()
        sum1[j] = added(sum0[j, mine1], rec1[j])
        copy2(j).start()

    def reduce2(j):
        copy2(j).wait()
        sum2[j] = added(sum1[j, mine2], rec2[j])
        for item in copy3(j):
            item.start()

    def update(j):
        copies = copy3(j)
        for item in copies:
            item.wait()
        summed = sum2[j, z].astype(jnp.float32)
        for k in range(zs - 1):
            summed = summed + rec3[j, k].astype(jnp.float32)
        own = pl.ds(pl.multiple_of((outer * inner_count + inner) * rows, rows), rows)
        for b in range(blocks):
            at = pl.ds(pl.multiple_of(j * width + b * block_len, block_len), block_len)
            gradient = (
                jnp.dot(
                    summed[:, b * block_len : (b + 1) * block_len],
                    matrix[...],
                    precision=highest,
                    preferred_element_type=jnp.float32,
                )
                * scale
                * signs[:, at]
            )
            new_master, _, _ = adam_update(
                gradient, master[:, at], first[:, at], second[:, at]
            )
            out_gradient[:, at] = gradient
            limit = diff_bounds[j, :, b : b + 1]
            change = new_master - base[own, at].astype(jnp.float32)
            change = jnp.minimum(jnp.maximum(change, -limit), limit)
            gath[j, c, mine1, mine2, z, :, b * block_len : (b + 1) * block_len] = change.astype(
                jnp.bfloat16
            )
        for item in gather0(j):
            item.start()

    def pass1(j):
        for item in gather0(j):
            item.wait()
        gather1(j).start()

    def pass2(j):
        gather1(j).wait()
        gather2(j).start()

    def pass3(j):
        gather2(j).wait()
        gather3(j).start()

    def consume(j):
        gather3(j).wait()
        for yy in range(2):
            for cc in range(2):
                group = yy * 2 + cc
                count = zs * xs * rows
                for zz in range(zs):
                    for xx in range(xs):
                        at1, at2 = (xx, yy) if cc == 0 else (yy, xx)
                        low = (zz * xs + xx) * rows
                        effective[low : low + rows, :] = added(
                            base[group * count + low : group * count + low + rows, columns(j)],
                            gath[j, cc, at1, at2, zz],
                        )
                total[:, group * count : (group + 1) * count] += lax.dot_general(
                    tokens[:, columns(j)],
                    effective[...],
                    (((1,), (1,)), ((), ())),
                    preferred_element_type=jnp.float32,
                )

    stages = (produce, reduce0, reduce1, reduce2, update, pass1, pass2, pass3, consume)

    def step(t, carry):
        for place, stage in enumerate(stages):
            j = t - place

            @pl.when((j >= 0) & (j < chunks))
            def _():
                stage(j)

        return carry

    lax.fori_loop(0, 4, step, 0)
    load_base.wait()
    lax.fori_loop(4, chunks + len(stages) - 1, step, 0)
    projected[...] = total[...].astype(jnp.bfloat16)


def fused_step(tokens, out_grad, master, base, first, second, bounds, diff_bounds, signs, matrix):
    rows, model_width = master.shape
    features = out_grad.shape[1]
    inner_count = lax.axis_size("inner")
    zs = inner_count // 2
    width = model_width // CHUNKS
    vmem = pl.BlockSpec(memory_space=pltpu.VMEM)
    half = jnp.bfloat16
    cell = (rows, width)
    flops = 4 * tokens.shape[0] * model_width * features
    projected, gradient = pl.pallas_call(
        functools.partial(step_kernel, CHUNKS),
        out_shape=(
            jax.ShapeDtypeStruct((tokens.shape[0], features), half),
            jax.ShapeDtypeStruct(master.shape, jnp.float32),
        ),
        in_specs=[vmem] * 3 + [pl.BlockSpec(memory_space=pl.ANY)] + [vmem] * 7,
        out_specs=(vmem,) * 2,
        scratch_shapes=[
            pltpu.VMEM(base.shape, half),
            pltpu.VMEM((features, tokens.shape[0]), half),
            pltpu.VMEM((CHUNKS, 2, 2, zs, 2) + cell, half),
            pltpu.VMEM((CHUNKS, 2, zs, 2) + cell, half),
            pltpu.VMEM((CHUNKS, 2, 2, zs) + cell, half),
            pltpu.VMEM((CHUNKS, 2, zs) + cell, half),
            pltpu.VMEM((CHUNKS, 2, zs) + cell, half),
            pltpu.VMEM((CHUNKS, zs) + cell, half),
            pltpu.VMEM((CHUNKS, zs) + cell, half),
            pltpu.VMEM((CHUNKS, zs - 1) + cell, half),
            pltpu.VMEM((CHUNKS, 2, 2, 2, zs) + cell, half),
            pltpu.VMEM((tokens.shape[0], width), half),
            pltpu.VMEM((features // 4, width), half),
            pltpu.VMEM((tokens.shape[0], features), jnp.float32),
            pltpu.SemaphoreType.DMA,
            pltpu.SemaphoreType.DMA((6, CHUNKS)),
            pltpu.SemaphoreType.DMA((6, CHUNKS)),
            pltpu.SemaphoreType.DMA((2, CHUNKS, zs - 1)),
            pltpu.SemaphoreType.DMA((2, CHUNKS, zs - 1)),
        ],
        compiler_params=pltpu.CompilerParams(
            collective_id=0, has_side_effects=True, vmem_limit_bytes=66000000
        ),
        cost_estimate=pl.CostEstimate(flops=flops, bytes_accessed=2**25, transcendentals=0),
    )(
        tokens,
        out_grad,
        master,
        base,
        first,
        second,
        bounds,
        diff_bounds,
        signs,
        jnp.asarray(matrix, half),
        jnp.asarray(matrix),
    )
    return (projected,) + adam_update(gradient, master, first, second)


def hadamard_constant(matrix_size):
    matrix = np.ones((1, 1), np.float32)
    while matrix.shape[0] < matrix_size:
        matrix = np.block([[matrix, matrix], [matrix, -matrix]])
    return matrix


def fits_kernel(token_rows, rows_dev, block_len, features, model_width):
    inner_count = lax.axis_size("inner")
    pair = 2 * rows_dev
    return (
        lax.axis_size("outer") == 4
        and inner_count % 2 == 0
        and inner_count > 2
        and rows_dev % 16 == 0
        and token_rows % 16 == 0
        and block_len % pair == 0
        and (inner_count * rows_dev) % block_len == 0
        and features == 4 * inner_count * rows_dev
        and model_width % (CHUNKS * block_len) == 0
        and features * model_width <= 2**22
    )


def shards(
    tokens,
    out_grad,
    master_weights,
    base_weights,
    adam_m,
    adam_v,
    grad_exps,
    diff_exps,
    hadamard_signs,
):
    outer_count = lax.axis_size("outer")
    inner_count = lax.axis_size("inner")
    token_rows = tokens.shape[0]
    model_width = tokens.shape[1]
    rows_dev = master_weights.shape[0]
    sign_rows = (2 * hadamard_signs - 1).astype(jnp.float32)
    block_len = sign_rows.shape[1]
    col_blocks = sign_rows.shape[0]
    matrix = hadamard(block_len)
    bound_all = jnp.repeat(
        clip_level * jnp.exp2(grad_exps[0].astype(jnp.float32)), block_len, axis=0
    )
    if fits_kernel(token_rows, rows_dev, block_len, out_grad.shape[1], model_width):
        limits = clip_level * jnp.exp2(grad_exps[0].astype(jnp.float32))
        diff_limits = clip_level * jnp.exp2(diff_exps.astype(jnp.float32))
        return fused_step(
            tokens,
            out_grad,
            master_weights,
            base_weights,
            adam_m,
            adam_v,
            jnp.repeat(limits, block_len, axis=1),
            diff_limits.reshape(rows_dev, CHUNKS, -1).transpose(1, 0, 2),
            sign_rows.reshape(1, -1),
            hadamard_constant(block_len),
        )
    grad_grid = out_grad.reshape(token_rows, outer_count, inner_count, rows_dev).transpose(
        0, 2, 1, 3
    )
    bound_grid = bound_all.reshape(outer_count, inner_count, rows_dev, col_blocks).transpose(
        1, 0, 2, 3
    )
    coded_bound_sel = bound_grid.reshape(-1, col_blocks)
    term_rows = lax.dot_general(
        grad_grid.reshape(token_rows, -1),
        tokens,
        (((0,), (0,)), ((), ())),
        preferred_element_type=jnp.float32,
    )
    turned = rotate_rows(term_rows, sign_rows, matrix)
    coded_rows = lax.optimization_barrier(clip_rows(turned, coded_bound_sel).astype(jnp.bfloat16))
    coded_rows = coded_rows.astype(jnp.float32)
    group_sum = lax.psum_scatter(
        coded_rows.reshape(1 * lax.axis_size("inner"), outer_count, rows_dev, model_width).astype(
            jnp.bfloat16
        ),
        "inner",
        scatter_dimension=0,
        tiled=True,
    )
    summed = (
        lax.psum_scatter(group_sum, "outer", scatter_dimension=1, tiled=True)
        .astype(jnp.float32)
        .reshape(rows_dev, model_width)
    )
    gradient = unrotate_rows(summed, sign_rows, matrix)
    new_master, new_first, new_second = adam_update(gradient, master_weights, adam_m, adam_v)
    owner = lax.axis_index("outer") * inner_count + lax.axis_index("inner")
    base_own = lax.dynamic_slice_in_dim(base_weights, owner * rows_dev, rows_dev, 0).astype(
        jnp.float32
    )
    diff_bound = clip_level * jnp.exp2(diff_exps.astype(jnp.float32))
    diff_coded = clip_rows(new_master - base_own, diff_bound).astype(jnp.bfloat16)
    effective = (
        base_weights.astype(jnp.float32)
        + lax.all_gather(diff_coded, ("outer", "inner"), axis=0, tiled=True).astype(jnp.float32)
    ).astype(jnp.bfloat16)
    result = lax.dot_general(
        tokens, effective, (((1,), (1,)), ((), ())), preferred_element_type=jnp.float32
    )
    projected = result.astype(jnp.bfloat16)
    return (projected, new_master, new_first, new_second)


def solution(mesh):
    in_specs = (
        P(("outer", "inner"), None),
        P(("outer", "inner"), None),
        P(("outer", "inner"), None),
        P(),
        P(("outer", "inner"), None),
        P(("outer", "inner"), None),
        P(("outer", "inner"), None, None),
        P(("outer", "inner"), None),
        P(),
    )
    out_specs = (
        P(("outer", "inner"), None),
        P(("outer", "inner"), None),
        P(("outer", "inner"), None),
        P(("outer", "inner"), None),
    )
    return jax.shard_map(shards, mesh=mesh, in_specs=in_specs, out_specs=out_specs, check_vma=False)
```

profile of v0, /device:TPU:0, one launch (start us, length us, event | category | flops | bytes accessed | tf_op | source)
XLA Modules:
  0.0 102.2 jit_solution(8912111263770410730)
XLA Ops:
  0.6 0.7 multiply_bitcast_fusion
  1.3 0.1 copy.16
  1.4 0.8 copy.17
  2.2 1.3 %add_convert_fusion = f32[32,128]{1,0:T(8,128)} fusion(s32[32,128]{1,0:T(8,128)} %param.19), kind=kLoop, calls=%fused_computation.5 | loop fusion | flops 12288 | bytes 32768 | tf_op jit(solution)/shard_map/convert_element_type | solution.py:427
  3.5 0.8 copy.18
  4.3 0.8 broadcast_bitcast_fusion.bounds
  5.1 0.0 copy-start
  5.1 92.3 %shard_map.138 = (bf16[384,1024]{1,0:T(8,128)(2,1)}, f32[32,4096]{1,0:T(8,128)}) custom-call(bf16[384,4096]{1,0:T(8,128)(2,1)} %tokens.1, bf16[384,1024]{1,0:T(8,128)(2,1)} %grad_rows.1, f32[32,4096]{1,0:T(8,128)} %master.1, bf16[1024,4096]{1,0:T(8,128)(2,1)} %base_hbm.1, f32[32,4096]{1,0:T(8,128)} %first.1, f32[32,4096]{1,0:T(8,128)} %second.1, ...), custom_call_target="tpu_custom_call" | custom-call | flops 6442450944 | bytes 33554432 | tf_op jit(solution)/shard_map/pallas_call | solution.py:338
  97.4 0.0 copy-done
  97.4 2.7 %multiply_subtract_fusion = (f32[32,4096]{1,0:T(8,128)}, f32[32,4096]{1,0:T(8,128)}, f32[32,4096]{1,0:T(8,128)}) fusion(f32[32,4096]{1,0:T(8,128)S(1)} %copy-done, f32[32,4096]{1,0:T(8,128)} %get-tuple-element.7, f32[32,4096]{1,0:T(8,128)} %first.1, f32[32,4096]{1,0:T(8,128)} %second.1), kind=kLoop, calls=%fused_computation.2 | loop fusion | flops 1966080 | bytes 3670016 | tf_op jit(solution)/shard_map/sub | solution.py:63
  100.2 2.1 %copy.20 = bf16[384,1024]{1,0:T(8,128)(2,1)} copy(bf16[384,1024]{1,0:T(8,128)(2,1)} %get-tuple-element.15) | data formatting | bytes 1572864
  (1 shorter events, 0.0 us)
Async XLA Ops:
  5.1 92.3 %copy-start = (f32[32,4096]{1,0:T(8,128)S(1)}, f32[32,4096]{1,0:T(8,128)}, u32[]{:S(2)}) copy-start(f32[32,4096]{1,0:T(8,128)} %master.1) | copy-start | bytes 1572868
where the time goes:
time: 103 us; the launch traced here: 102 us
  Pallas kernels  92.3 us (90%)
  other arithmetic  4.78 us (5%)
  local copies, waits for them, and re-layouts  4.47 us (4%)
    pallas_call x1, Pallas kernels, fused_step(): pl.pallas_call(functools.partial(step_kernel, CHUNKS), out_shape=(jax.Sha...  92.3 us
    unnamed x4, local copies, waits for them, and re-layouts  2.86 us
    sub x1, other arithmetic, adam_update(): new_master = master - learn_rate * (step_dir + decay_rate * master)  2.75 us

commit v1 on v0

v1 whole, which is shorter than its diff:
```python
import functools
import math

import jax
import jax.numpy as jnp
import numpy as np
from jax import lax
from jax.experimental import pallas as pl
from jax.experimental.pallas import tpu as pltpu
from jax.sharding import PartitionSpec as P

ADAM_STEP = 10


clip_level = 448.0
beta_one = 0.9
beta_two = 0.95
learn_rate = 0.002
decay_rate = 0.1
adam_eps = 1e-08
highest = lax.Precision.HIGHEST


def hadamard(matrix_size):
    positions = jnp.arange(matrix_size, dtype=jnp.int32)
    common = positions[:, None] & positions[None, :]
    parity = jnp.zeros((matrix_size, matrix_size), jnp.int32)
    for bit_level in range(matrix_size.bit_length() - 1):
        parity = parity + (common >> bit_level & 1)
    return (1 - 2 * (parity % 2)).astype(jnp.float32)


def rotate_rows(row_block, sign_rows, matrix):
    row_count = row_block.shape[0]
    blocks = row_block.reshape(row_count, sign_rows.shape[0], sign_rows.shape[1]) * sign_rows
    turned = jnp.dot(blocks.reshape(-1, sign_rows.shape[1]), matrix, precision=highest)
    return turned.reshape(row_block.shape) / math.sqrt(sign_rows.shape[1])


def unrotate_rows(row_block, sign_rows, matrix):
    row_count = row_block.shape[0]
    turned = jnp.dot(
        row_block.reshape(-1, sign_rows.shape[1]), matrix, precision=highest
    ) / math.sqrt(sign_rows.shape[1])
    return (turned.reshape(row_count, sign_rows.shape[0], sign_rows.shape[1]) * sign_rows).reshape(
        row_block.shape
    )


def clip_rows(row_block, bound_rows):
    row_count = row_block.shape[0]
    shaped = row_block.reshape(row_count, bound_rows.shape[1], -1)
    limits = bound_rows[:, :, None]
    return jnp.clip(shaped, -limits, limits).reshape(row_block.shape)


def adam_update(gradient, master, first, second):
    new_first = beta_one * first + (1.0 - beta_one) * gradient
    new_second = beta_two * second + (1.0 - beta_two) * gradient * gradient
    fix_one = 1.0 - beta_one**ADAM_STEP
    fix_two = 1.0 - beta_two**ADAM_STEP
    step_dir = new_first / fix_one / (jnp.sqrt(new_second / fix_two) + adam_eps)
    new_master = master - learn_rate * (step_dir + decay_rate * master)
    return (new_master, new_first, new_second)


CHUNKS = 16
VMEM_LIMIT = 58000000
DELAYS = (-3, 1, 3, 5, 7, 9, 11, 13, 15, 17, 18)


def z_turn(j):
    return 1 + j % 2


MESH = pl.DeviceIdType.MESH


def step_kernel(
    chunks,
    delays,
    tokens_hbm,
    grad_hbm,
    master_hbm,
    base_hbm,
    first_hbm,
    second_hbm,
    grad_exps_hbm,
    diff_exps_hbm,
    signs_hbm,
    matrix_hbm,
    projected,
    out_master,
    out_first,
    out_second,
    tokens,
    grad_rows,
    master,
    base,
    first,
    second,
    grad_exps,
    diff_exps,
    sign_bits,
    matrix,
    bounds,
    diff_bounds,
    signs,
    grad_t,
    coded,
    rec0,
    sum0,
    rec1,
    sum1,
    rec2,
    sum2,
    rec3,
    sum3,
    rec4,
    gath,
    effective,
    total,
    load_sem,
    send_sem,
    recv_sem,
):
    outer, inner = lax.axis_index("outer"), lax.axis_index("inner")
    xs = 2
    y, c = outer // 2, outer % 2
    z, x = inner // xs, inner % xs
    zh, zl = z // 2, z % 2
    rows = master.shape[0]
    half = grad_t.shape[1]
    width = tokens.shape[1] // chunks
    block_len = sign_bits.shape[1]
    blocks = width // block_len
    groups = half // block_len
    scale = 1.0 / math.sqrt(block_len)
    ahead = 1 - delays[0]
    core_peer = (y * 2 + 1 - c, inner)
    x_peer = (outer, z * xs + 1 - x)
    y_peer = ((1 - y) * 2 + c, inner)
    near_peer = (outer, (zh * 2 + 1 - zl) * xs + x)
    far_peer = (outer, ((1 - zh) * 2 + zl) * xs + x)

    def turns(j, h, along_x, along_y, along_z):
        turn = z_turn(j)
        on0 = (2 - turn) * (1 - turn) // 2
        on1 = turn * (2 - turn)
        on2 = turn * (turn - 1) // 2
        lead = along_x * (1 - h) + along_y * h
        trail = along_y * (1 - h) + along_x * h
        return (
            along_z * on0 + lead * (1 - on0),
            along_z * on1 + lead * on0 + trail * on2,
            along_z * on2 + trail * (1 - on2),
        )

    def mine(j):
        return turns(j, c, x, y, zl) + (zh,)

    def peer_of(j, at):
        if at == 3:
            return far_peer
        return tuple(
            turns(j, c, *ids)[at] for ids in zip(x_peer, y_peer, near_peer)
        )

    barrier = pltpu.get_barrier_semaphore()
    peers = [core_peer, x_peer, y_peer, near_peer, far_peer]
    for peer in peers:
        pl.semaphore_signal(barrier, inc=1, device_id=peer, device_id_type=MESH)

    def load(src, dst, at):
        return pltpu.make_async_copy(src, dst, load_sem.at[at])

    head = pl.ds(0, width)
    tail = pl.ds(width, tokens.shape[1] - width)
    load_grad = load(grad_hbm, grad_rows, 0)
    load_signs = load(signs_hbm, sign_bits, 1)
    load_matrix = load(matrix_hbm, matrix, 2)
    load_head = load(tokens_hbm.at[:, head], tokens.at[:, head], 3)
    load_grad_exps = load(grad_exps_hbm, grad_exps, 4)
    load_tail = load(tokens_hbm.at[:, tail], tokens.at[:, tail], 5)
    late = [
        load(diff_exps_hbm, diff_exps, 6),
        load(master_hbm, master, 7),
        load(first_hbm, first, 8),
        load(second_hbm, second, 9),
        load(base_hbm, base, 10),
    ]
    for item in [load_grad, load_signs, load_matrix, load_head, load_grad_exps, load_tail] + late:
        item.start()

    load_grad.wait()
    for h in range(2):
        for yy in range(2):
            low = (yy * 2 + h) * (half // 2)
            grad_t[h, yy * (half // 2) : (yy + 1) * (half // 2), :] = grad_rows[
                :, low : low + half // 2
            ].T
    load_signs.wait()
    load_matrix.wait()
    load_grad_exps.wait()
    limits = clip_level * jnp.exp2(grad_exps[...].astype(jnp.float32))
    for b in range(sign_bits.shape[0]):
        at = slice(b * block_len, (b + 1) * block_len)
        signs[:, at] = (2 * sign_bits[b : b + 1, :] - 1).astype(jnp.float32)
        bounds[:, at] = jnp.broadcast_to(
            limits[:, b : b + 1], (limits.shape[0], block_len)
        )
    load_head.wait()

    def remote(src, dst, stage, j, peer):
        return pltpu.make_async_remote_copy(
            src_ref=src,
            dst_ref=dst,
            send_sem=send_sem.at[stage, j],
            recv_sem=recv_sem.at[stage, j],
            device_id=peer,
            device_id_type=MESH,
        )

    def copy0(j):
        return remote(coded.at[j, 1 - c], rec0.at[j], 0, j, core_peer)

    def copy1(j):
        return remote(sum0.at[j, 1 - mine(j)[0]], rec1.at[j], 1, j, peer_of(j, 0))

    def copy2(j):
        return remote(sum1.at[j, 1 - mine(j)[1]], rec2.at[j], 2, j, peer_of(j, 1))

    def copy3(j):
        return remote(sum2.at[j, 1 - mine(j)[2]], rec3.at[j], 3, j, peer_of(j, 2))

    def copy4(j):
        return remote(sum3.at[j, 1 - mine(j)[3]], rec4.at[j], 4, j, peer_of(j, 3))

    def gather4(j):
        m = mine(j)
        block = gath.at[j, c, m[0], m[1], m[2], m[3]]
        return remote(block, block, 5, j, peer_of(j, 3))

    def gather3(j):
        m = mine(j)
        block = gath.at[j, c, m[0], m[1], m[2]]
        return remote(block, block, 6, j, peer_of(j, 2))

    def gather2(j):
        m = mine(j)
        block = gath.at[j, c, m[0], m[1]]
        return remote(block, block, 7, j, peer_of(j, 1))

    def gather1(j):
        block = gath.at[j, c, mine(j)[0]]
        return remote(block, block, 8, j, peer_of(j, 0))

    def gather0(j):
        block = gath.at[j, c]
        return remote(block, block, 9, j, core_peer)

    def columns(j):
        return pl.ds(pl.multiple_of(j * width, width), width)

    def produce(j, send=True):
        rotated = jnp.dot(
            tokens[:, columns(j)] * signs[:, columns(j)].astype(jnp.bfloat16),
            matrix[...],
            preferred_element_type=jnp.float32,
        )
        rotated = (rotated * scale).astype(jnp.bfloat16)
        for h in (1 - c, c):
            part = jnp.dot(grad_t[h], rotated, preferred_element_type=jnp.float32)
            for g in range(groups):
                yy, hh = g // 2, g % 2
                limit = bounds[pl.ds(yy * 4 + h * 2 + hh, 1), columns(j)]
                piece = part[g * block_len : (g + 1) * block_len, :]
                piece = jnp.minimum(jnp.maximum(piece, -limit), limit).astype(jnp.bfloat16)
                coded[j, h, yy, hh] = piece.reshape(2, xs, rows, width)
            if send and h is not c:
                copy0(j).start()

    def reduce0(j):
        copy0(j).wait()
        for yy in range(2):
            for hh in range(2):
                for ll in range(2):
                    for xx in range(xs):
                        to1, to2, to3 = turns(j, c, xx, yy, ll)
                        sum0[j, to1, to2, to3, hh] = (
                            coded[j, c, yy, hh, ll, xx] + rec0[j, yy, hh, ll, xx]
                        )
        copy1(j).start()

    def reduce1(j):
        copy1(j).wait()
        sum1[j] = sum0[j, mine(j)[0]] + rec1[j]
        copy2(j).start()

    def reduce2(j):
        copy2(j).wait()
        sum2[j] = sum1[j, mine(j)[1]] + rec2[j]
        copy3(j).start()

    def reduce3(j):
        copy3(j).wait()
        sum3[j] = sum2[j, mine(j)[2]] + rec3[j]
        copy4(j).start()

    def update(j):
        copy4(j).wait()
        summed = sum3[j, zh].astype(jnp.float32) + rec4[j].astype(jnp.float32)
        high = summed.astype(jnp.bfloat16)
        rest = summed - high.astype(jnp.float32)
        middle = rest.astype(jnp.bfloat16)
        low = (rest - middle.astype(jnp.float32)).astype(jnp.bfloat16)
        turned = jnp.dot(
            jnp.concatenate([high, middle, low], axis=0),
            matrix[...],
            preferred_element_type=jnp.float32,
        )
        gradient = (turned[:rows] + turned[rows : 2 * rows]) + turned[2 * rows :]
        gradient = gradient * scale * signs[:, columns(j)]
        own = pl.ds(pl.multiple_of((outer * 8 + inner) * rows, rows), rows)
        new_master, new_first, new_second = adam_update(
            gradient, master[:, columns(j)], first[:, columns(j)], second[:, columns(j)]
        )
        out_master[:, columns(j)] = new_master
        out_first[:, columns(j)] = new_first
        out_second[:, columns(j)] = new_second
        limit = diff_bounds[:, columns(j)]
        change = new_master - base[own, columns(j)].astype(jnp.float32)
        change = jnp.minimum(jnp.maximum(change, -limit), limit)
        m = mine(j)
        gath[j, c, m[0], m[1], m[2], m[3]] = change.astype(jnp.bfloat16)
        gather4(j).start()

    def pass3(j):
        gather4(j).wait()
        gather3(j).start()

    def pass2(j):
        gather3(j).wait()
        gather2(j).start()

    def pass1(j):
        gather2(j).wait()
        gather1(j).start()

    def consume(j, h):
        for yy in range(2):
            for hh in range(2):
                for ll in range(2):
                    for xx in range(xs):
                        at1, at2, at3 = turns(j, h, xx, yy, ll)
                        low = ((yy * 4 + h * 2 + hh) * 4 + ll * 2 + xx) * rows
                        spot = ((yy * 2 + hh) * 4 + ll * 2 + xx) * rows
                        effective[spot : spot + rows, :] = (
                            base[pl.ds(pl.multiple_of(low, rows), rows), columns(j)]
                            + gath[j, h, at1, at2, at3, hh]
                        )
        total[h] += lax.dot_general(
            tokens[:, columns(j)],
            effective[...],
            (((1,), (1,)), ((), ())),
            preferred_element_type=jnp.float32,
        )

    def pass0(j):
        gather1(j).wait()
        gather0(j).start()
        consume(j, c)

    def last(j):
        gather0(j).wait()
        consume(j, 1 - c)

    stages = (
        produce,
        reduce0,
        reduce1,
        reduce2,
        reduce3,
        update,
        pass3,
        pass2,
        pass1,
        pass0,
        last,
    )
    order = (1, 2, 3, 4, 5, 6, 7, 8, 9, 0, 10)

    def step(t, carry):
        for at in order:
            j = t - delays[at]

            @pl.when((j >= 0) & (j < chunks))
            def _():
                stages[at](j)

        return carry

    load_tail.wait()

    def early(j, carry):
        produce(j, send=False)
        return carry

    lax.fori_loop(0, ahead, early, 0)
    pl.semaphore_wait(barrier, len(peers))

    def sent(j, carry):
        copy0(j).start()
        return carry

    lax.fori_loop(0, ahead, sent, 0)
    total[...] = jnp.zeros_like(total)
    late[0].wait()
    spans = clip_level * jnp.exp2(diff_exps[...].astype(jnp.float32))
    for b in range(sign_bits.shape[0]):
        at = slice(b * block_len, (b + 1) * block_len)
        diff_bounds[:, at] = jnp.broadcast_to(spans[:, b : b + 1], (rows, block_len))
    start = min(delays[5], 3)
    lax.fori_loop(1, start, step, 0)
    for item in late[1:]:
        item.wait()
    lax.fori_loop(start, chunks + max(delays), step, 0)
    for h in range(2):
        for yy in range(2):
            low = (yy * 2 + h) * (half // 2)
            projected[:, low : low + half // 2] = total[
                h, :, yy * (half // 2) : (yy + 1) * (half // 2)
            ].astype(jnp.bfloat16)


def write_kernel(*refs):
    sources, targets, sems = refs[:4], refs[4:8], refs[8]
    copies = [
        pltpu.make_async_copy(source, target, sems.at[at])
        for at, (source, target) in enumerate(zip(sources, targets))
    ]
    for item in copies:
        item.start()
    for item in copies:
        item.wait()


def fused_step(
    tokens, out_grad, master, base, first, second, grad_exps, diff_exps, sign_bits, matrix
):
    rows, model_width = master.shape
    token_rows, features = out_grad.shape
    matrix_len = matrix.shape[0]
    width = model_width // CHUNKS
    anywhere = pl.BlockSpec(memory_space=pltpu.HBM)
    vmem = pl.BlockSpec(memory_space=pltpu.VMEM)
    half = jnp.bfloat16
    cell = (rows, width)
    flops = 4 * token_rows * model_width * features
    matrix = jnp.asarray(np.kron(np.eye(width // matrix.shape[0]), matrix), half)
    operands = (
        tokens, out_grad, master, base, first, second, grad_exps, diff_exps, sign_bits, matrix
    )
    results = pl.pallas_call(
        functools.partial(step_kernel, CHUNKS, DELAYS),
        out_shape=(
            pltpu.VMEM((token_rows, features), half),
            pltpu.VMEM(master.shape, jnp.float32),
            pltpu.VMEM(master.shape, jnp.float32),
            pltpu.VMEM(master.shape, jnp.float32),
        ),
        in_specs=[anywhere] * len(operands),
        out_specs=(vmem,) * 4,
        scratch_shapes=[pltpu.VMEM(item.shape, item.dtype) for item in operands]
        + [
            pltpu.VMEM((features // matrix_len, model_width), jnp.float32),
            pltpu.VMEM(master.shape, jnp.float32),
            pltpu.VMEM((1, model_width), jnp.float32),
            pltpu.VMEM((2, features // 2, token_rows), half),
            pltpu.VMEM((CHUNKS, 2, 2, 2, 2, 2) + cell, half),
            pltpu.VMEM((CHUNKS, 2, 2, 2, 2) + cell, half),
            pltpu.VMEM((CHUNKS, 2, 2, 2, 2) + cell, half),
            pltpu.VMEM((CHUNKS, 2, 2, 2) + cell, half),
            pltpu.VMEM((CHUNKS, 2, 2, 2) + cell, half),
            pltpu.VMEM((CHUNKS, 2, 2) + cell, half),
            pltpu.VMEM((CHUNKS, 2, 2) + cell, half),
            pltpu.VMEM((CHUNKS, 2) + cell, half),
            pltpu.VMEM((CHUNKS, 2) + cell, half),
            pltpu.VMEM((CHUNKS,) + cell, half),
            pltpu.VMEM((CHUNKS, 2, 2, 2, 2, 2) + cell, half),
            pltpu.VMEM((features // 2, width), half),
            pltpu.VMEM((2, token_rows, features // 2), jnp.float32),
            pltpu.SemaphoreType.DMA((11,)),
            pltpu.SemaphoreType.DMA((10, CHUNKS)),
            pltpu.SemaphoreType.DMA((10, CHUNKS)),
        ],
        compiler_params=pltpu.CompilerParams(
            collective_id=0, has_side_effects=True, vmem_limit_bytes=VMEM_LIMIT
        ),
        cost_estimate=pl.CostEstimate(flops=flops, bytes_accessed=2**25, transcendentals=0),
    )(*operands)
    return pl.pallas_call(
        write_kernel,
        out_shape=tuple(jax.ShapeDtypeStruct(item.shape, item.dtype) for item in results),
        in_specs=[vmem] * 4,
        out_specs=(anywhere,) * 4,
        scratch_shapes=[pltpu.SemaphoreType.DMA((4,))],
    )(*[pltpu.with_memory_space_constraint(item, pltpu.VMEM) for item in results])


def hadamard_constant(matrix_size):
    matrix = np.ones((1, 1), np.float32)
    while matrix.shape[0] < matrix_size:
        matrix = np.block([[matrix, matrix], [matrix, -matrix]])
    return matrix


def fits_kernel(token_rows, rows_dev, block_len, features, model_width):
    return (
        lax.axis_size("outer") == 4
        and lax.axis_size("inner") == 8
        and rows_dev % 16 == 0
        and token_rows % 16 == 0
        and block_len == 4 * rows_dev
        and features == 32 * rows_dev
        and model_width % (CHUNKS * block_len) == 0
        and features * model_width <= 2**22
        and token_rows <= 384
    )


def shards(
    tokens,
    out_grad,
    master_weights,
    base_weights,
    adam_m,
    adam_v,
    grad_exps,
    diff_exps,
    hadamard_signs,
):
    outer_count = lax.axis_size("outer")
    inner_count = lax.axis_size("inner")
    token_rows = tokens.shape[0]
    model_width = tokens.shape[1]
    rows_dev = master_weights.shape[0]
    sign_rows = (2 * hadamard_signs - 1).astype(jnp.float32)
    block_len = sign_rows.shape[1]
    col_blocks = sign_rows.shape[0]
    matrix = hadamard(block_len)
    bound_all = jnp.repeat(
        clip_level * jnp.exp2(grad_exps[0].astype(jnp.float32)), block_len, axis=0
    )
    if fits_kernel(token_rows, rows_dev, block_len, out_grad.shape[1], model_width):
        return fused_step(
            tokens,
            out_grad,
            master_weights,
            base_weights,
            adam_m,
            adam_v,
            grad_exps[0],
            diff_exps,
            hadamard_signs,
            hadamard_constant(block_len),
        )
    grad_grid = out_grad.reshape(token_rows, outer_count, inner_count, rows_dev).transpose(
        0, 2, 1, 3
    )
    bound_grid = bound_all.reshape(outer_count, inner_count, rows_dev, col_blocks).transpose(
        1, 0, 2, 3
    )
    coded_bound_sel = bound_grid.reshape(-1, col_blocks)
    term_rows = lax.dot_general(
        grad_grid.reshape(token_rows, -1),
        tokens,
        (((0,), (0,)), ((), ())),
        preferred_element_type=jnp.float32,
    )
    turned = rotate_rows(term_rows, sign_rows, matrix)
    coded_rows = lax.optimization_barrier(clip_rows(turned, coded_bound_sel).astype(jnp.bfloat16))
    coded_rows = coded_rows.astype(jnp.float32)
    group_sum = lax.psum_scatter(
        coded_rows.reshape(1 * lax.axis_size("inner"), outer_count, rows_dev, model_width).astype(
            jnp.bfloat16
        ),
        "inner",
        scatter_dimension=0,
        tiled=True,
    )
    summed = (
        lax.psum_scatter(group_sum, "outer", scatter_dimension=1, tiled=True)
        .astype(jnp.float32)
        .reshape(rows_dev, model_width)
    )
    gradient = unrotate_rows(summed, sign_rows, matrix)
    new_master, new_first, new_second = adam_update(gradient, master_weights, adam_m, adam_v)
    owner = lax.axis_index("outer") * inner_count + lax.axis_index("inner")
    base_own = lax.dynamic_slice_in_dim(base_weights, owner * rows_dev, rows_dev, 0).astype(
        jnp.float32
    )
    diff_bound = clip_level * jnp.exp2(diff_exps.astype(jnp.float32))
    diff_coded = clip_rows(new_master - base_own, diff_bound).astype(jnp.bfloat16)
    effective = (
        base_weights.astype(jnp.float32)
        + lax.all_gather(diff_coded, ("outer", "inner"), axis=0, tiled=True).astype(jnp.float32)
    ).astype(jnp.bfloat16)
    result = lax.dot_general(
        tokens, effective, (((1,), (1,)), ((), ())), preferred_element_type=jnp.float32
    )
    projected = result.astype(jnp.bfloat16)
    return (projected, new_master, new_first, new_second)


def solution(mesh):
    in_specs = (
        P(("outer", "inner"), None),
        P(("outer", "inner"), None),
        P(("outer", "inner"), None),
        P(),
        P(("outer", "inner"), None),
        P(("outer", "inner"), None),
        P(("outer", "inner"), None, None),
        P(("outer", "inner"), None),
        P(),
    )
    out_specs = (
        P(("outer", "inner"), None),
        P(("outer", "inner"), None),
        P(("outer", "inner"), None),
        P(("outer", "inner"), None),
    )
    return jax.shard_map(shards, mesh=mesh, in_specs=in_specs, out_specs=out_specs, check_vma=False)
```

time: 103 us -> 83.6 us (0.81)
  Pallas kernels: 92.3 us -> 82.8 us
  other arithmetic: 4.78 us -> 0 us
  local copies, waits for them, and re-layouts: 4.47 us -> 0 us
    pallas_call x1 -> x2, Pallas kernels: 92.3 us -> 82.8 us  [the longest x1 81.4 us: fused_step(): pl.pallas_call(functools.partial(step_kernel, CHUNKS, DELAYS), out_shape=...]
    unnamed x4 -> x0, local copies, waits for them, and re-layouts: 2.86 us -> none
    sub x1 -> x0, other arithmetic: 2.75 us -> none  [adam_update(): new_master = master - learn_rate * (step_dir + decay_rate * master)]
    reshape x2 -> x0, local copies, waits for them, and re-layouts: 1.54 us -> none  [the longest x1 0.78 us: shards(): diff_limits.reshape(rows_dev, CHUNKS, -1).transpose(1, 0, 2)]
    convert_element_type x1 -> x0, other arithmetic: 1.33 us -> none  [shards(): sign_rows = (2 * hadamard_signs - 1).astype(jnp.float32)]
where the time goes in v1:
time: 83.6 us; the launch traced here: 83.5 us
  Pallas kernels  82.8 us (99%)
    pallas_call x1, Pallas kernels, fused_step(): pl.pallas_call(functools.partial(step_kernel, CHUNKS, DELAYS), out_shape=...  81.4 us

profile of v1, /device:TPU:0, one launch (start us, length us, event | category | flops | bytes accessed | tf_op | source)
XLA Modules:
  0.0 83.5 jit_solution(6580790466267499997)
XLA Ops:
  0.6 81.4 %shard_map.129 = (bf16[384,1024]{1,0:T(8,128)(2,1)S(1)}, f32[32,4096]{1,0:T(8,128)S(1)}, f32[32,4096]{1,0:T(8,128)S(1)}, f32[32,4096]{1,0:T(8,128)S(1)}) custom-call(bf16[384,4096]{1,0:T(8,128)(2,1)} %tokens_hbm.1, bf16[384,1024]{1,0:T(8,128)(2,1)} %grad_hbm.1, f32[32,4096]{1,0:T(8,128)} %master_hbm.1, bf16[1024,4096]{1,0:T(8,128)(2,1)} %base_hbm.1, ...), custom_call_target="tpu_custom_call" | custom-call | flops 6442450944 | bytes 33554432 | tf_op jit(solution)/shard_map/pallas_call | solution.py:464
  82.0 1.4 %shard_map.130 = (bf16[384,1024]{1,0:T(8,128)(2,1)}, f32[32,4096]{1,0:T(8,128)}, f32[32,4096]{1,0:T(8,128)}, f32[32,4096]{1,0:T(8,128)}) custom-call(bf16[384,1024]{1,0:T(8,128)(2,1)S(1)} %get-tuple-element.8.refs_0_, f32[32,4096]{1,0:T(8,128)S(1)} %get-tuple-element.9.refs_1_, f32[32,4096]{1,0:T(8,128)S(1)} %get-tuple-element.10.refs_2_, ...), custom_call_target="tpu_custom_call" | custom-call | tf_op jit(solution)/shard_map/pallas_call | solution.py:502

commit v2 on v1

--- a/solution.py
+++ b/solution.py
@@ -65,8 +65,9 @@
 
 
 CHUNKS = 16
+PAIR = 2
 VMEM_LIMIT = 58000000
-DELAYS = (-3, 1, 3, 5, 7, 9, 11, 13, 15, 17, 18)
+DELAYS = (-3, 1, 3, 5, 7, 9, 11, 13, 15, 18, 19)
 
 
 def z_turn(j):
@@ -136,6 +137,7 @@
     blocks = width // block_len
     groups = half // block_len
     scale = 1.0 / math.sqrt(block_len)
+    pair = effective.shape[1] // width
     ahead = 1 - delays[0]
     core_peer = (y * 2 + 1 - c, inner)
     x_peer = (outer, z * xs + 1 - x)
@@ -348,23 +350,31 @@
         gather1(j).start()
 
     def consume(j, h):
-        for yy in range(2):
-            for hh in range(2):
-                for ll in range(2):
-                    for xx in range(xs):
-                        at1, at2, at3 = turns(j, h, xx, yy, ll)
-                        low = ((yy * 4 + h * 2 + hh) * 4 + ll * 2 + xx) * rows
-                        spot = ((yy * 2 + hh) * 4 + ll * 2 + xx) * rows
-                        effective[spot : spot + rows, :] = (
-                            base[pl.ds(pl.multiple_of(low, rows), rows), columns(j)]
-                            + gath[j, h, at1, at2, at3, hh]
-                        )
-        total[h] += lax.dot_general(
-            tokens[:, columns(j)],
-            effective[...],
-            (((1,), (1,)), ((), ())),
-            preferred_element_type=jnp.float32,
-        )
+        @pl.when(j % pair == pair - 1)
+        def _():
+            first_chunk = j - (pair - 1)
+            for k in range(pair):
+                for yy in range(2):
+                    for hh in range(2):
+                        for ll in range(2):
+                            for xx in range(xs):
+                                at1, at2, at3 = turns(first_chunk + k, h, xx, yy, ll)
+                                low = ((yy * 4 + h * 2 + hh) * 4 + ll * 2 + xx) * rows
+                                spot = ((yy * 2 + hh) * 4 + ll * 2 + xx) * rows
+                                effective[spot : spot + rows, k * width : (k + 1) * width] = (
+                                    base[
+                                        pl.ds(pl.multiple_of(low, rows), rows),
+                                        columns(first_chunk + k),
+                                    ]
+                                    + gath[first_chunk + k, h, at1, at2, at3, hh]
+                                )
+            span = pl.ds(pl.multiple_of(first_chunk * width, pair * width), pair * width)
+            total[h] += lax.dot_general(
+                tokens[:, span],
+                effective[...],
+                (((1,), (1,)), ((), ())),
+                preferred_element_type=jnp.float32,
+            )
 
     def pass0(j):
         gather1(j).wait()
@@ -452,6 +462,7 @@
     token_rows, features = out_grad.shape
     matrix_len = matrix.shape[0]
     width = model_width // CHUNKS
+    pair = PAIR
     anywhere = pl.BlockSpec(memory_space=pltpu.HBM)
     vmem = pl.BlockSpec(memory_space=pltpu.VMEM)
     half = jnp.bfloat16
@@ -488,7 +499,7 @@
             pltpu.VMEM((CHUNKS, 2) + cell, half),
             pltpu.VMEM((CHUNKS,) + cell, half),
             pltpu.VMEM((CHUNKS, 2, 2, 2, 2, 2) + cell, half),
-            pltpu.VMEM((features // 2, width), half),
+            pltpu.VMEM((features // 2, pair * width), half),
             pltpu.VMEM((2, token_rows, features // 2), jnp.float32),
             pltpu.SemaphoreType.DMA((11,)),
             pltpu.SemaphoreType.DMA((10, CHUNKS)),

time: 83.6 us -> 82.1 us (0.982)
  Pallas kernels: 82.8 us -> 81.3 us
    pallas_call x1, Pallas kernels: 81.4 us -> 79.9 us  [fused_step(): pl.pallas_call(functools.partial(step_kernel, CHUNKS, DELAYS), out_shape=...]
where the time goes in v2:
time: 82.1 us; the launch traced here: 81.9 us
  Pallas kernels  81.3 us (99%)
    pallas_call x1, Pallas kernels, fused_step(): pl.pallas_call(functools.partial(step_kernel, CHUNKS, DELAYS), out_shape=...  79.9 us

profile of v2, /device:TPU:0, one launch (start us, length us, event | category | flops | bytes accessed | tf_op | source)
XLA Modules:
  0.0 81.9 jit_solution(16697189000849343106)
XLA Ops:
  0.6 79.9 %shard_map.129 = (bf16[384,1024]{1,0:T(8,128)(2,1)S(1)}, f32[32,4096]{1,0:T(8,128)S(1)}, f32[32,4096]{1,0:T(8,128)S(1)}, f32[32,4096]{1,0:T(8,128)S(1)}) custom-call(bf16[384,4096]{1,0:T(8,128)(2,1)} %tokens_hbm.1, bf16[384,1024]{1,0:T(8,128)(2,1)} %grad_hbm.1, f32[32,4096]{1,0:T(8,128)} %master_hbm.1, bf16[1024,4096]{1,0:T(8,128)(2,1)} %base_hbm.1, ...), custom_call_target="tpu_custom_call" | custom-call | flops 6442450944 | bytes 33554432 | tf_op jit(solution)/shard_map/pallas_call | solution.py:475
  80.5 1.4 %shard_map.130 = (bf16[384,1024]{1,0:T(8,128)(2,1)}, f32[32,4096]{1,0:T(8,128)}, f32[32,4096]{1,0:T(8,128)}, f32[32,4096]{1,0:T(8,128)}) custom-call(bf16[384,1024]{1,0:T(8,128)(2,1)S(1)} %get-tuple-element.8.refs_0_, f32[32,4096]{1,0:T(8,128)S(1)} %get-tuple-element.9.refs_1_, f32[32,4096]{1,0:T(8,128)S(1)} %get-tuple-element.10.refs_2_, ...), custom_call_target="tpu_custom_call" | custom-call | tf_op jit(solution)/shard_map/pallas_call | solution.py:513

commit v3 on v2

--- a/solution.py
+++ b/solution.py
@@ -67,7 +67,7 @@
 CHUNKS = 16
 PAIR = 2
 VMEM_LIMIT = 58000000
-DELAYS = (-3, 1, 3, 5, 7, 9, 11, 13, 15, 18, 19)
+DELAYS = (-1, 1, 3, 5, 7, 9, 11, 13, 15, 18, 19)
 
 
 def z_turn(j):

time: 82.1 us -> 81.4 us (level)
  no operation moved by 1% of the time
where the time goes in v3:
time: 81.4 us; the launch traced here: 81.2 us
  Pallas kernels  80.6 us (99%)
    pallas_call x1, Pallas kernels, fused_step(): pl.pallas_call(functools.partial(step_kernel, CHUNKS, DELAYS), out_shape=...  79.1 us

profile of v3, /device:TPU:0, one launch (start us, length us, event | category | flops | bytes accessed | tf_op | source)
XLA Modules:
  0.0 81.2 jit_solution(1203887750055634011)
XLA Ops:
  0.6 79.1 %shard_map.129 = (bf16[384,1024]{1,0:T(8,128)(2,1)S(1)}, f32[32,4096]{1,0:T(8,128)S(1)}, f32[32,4096]{1,0:T(8,128)S(1)}, f32[32,4096]{1,0:T(8,128)S(1)}) custom-call(bf16[384,4096]{1,0:T(8,128)(2,1)} %tokens_hbm.1, bf16[384,1024]{1,0:T(8,128)(2,1)} %grad_hbm.1, f32[32,4096]{1,0:T(8,128)} %master_hbm.1, bf16[1024,4096]{1,0:T(8,128)(2,1)} %base_hbm.1, ...), custom_call_target="tpu_custom_call" | custom-call | flops 6442450944 | bytes 33554432 | tf_op jit(solution)/shard_map/pallas_call | solution.py:475
  79.8 1.4 %shard_map.130 = (bf16[384,1024]{1,0:T(8,128)(2,1)}, f32[32,4096]{1,0:T(8,128)}, f32[32,4096]{1,0:T(8,128)}, f32[32,4096]{1,0:T(8,128)}) custom-call(bf16[384,1024]{1,0:T(8,128)(2,1)S(1)} %get-tuple-element.8.refs_0_, f32[32,4096]{1,0:T(8,128)S(1)} %get-tuple-element.9.refs_1_, f32[32,4096]{1,0:T(8,128)S(1)} %get-tuple-element.10.refs_2_, ...), custom_call_target="tpu_custom_call" | custom-call | tf_op jit(solution)/shard_map/pallas_call | solution.py:513
